TPU v7x, 256 devices: a whole 4x4x8 slice. The times are simulated.
256 devices in a mesh: ctx: 32 (over y_hi, z, core), tp: 8 (over y_lo, x).
Axes of the slice: x: 4, y: 4 (y_hi: 2, y_lo: 2; y = y_hi * 2 + y_lo), z: 8, core: 2. Of those that a mesh axis runs over, the one named last changes fastest.
Arguments:
- tokens: bfloat16 [8192, 8192], P(('ctx', 'tp')), may hold values from -64 to 64
- query_weight: bfloat16 [8192, 4096], P(None, 'tp'), may hold values from -0.0625 to 0.0625
- keyval_weight: bfloat16 [8192, 2048], P(None, 'tp'), may hold values from -0.0625 to 0.0625
- doc_lengths: int32 [64], replicated, may hold values from 1 to 2048, 8192 in all
- owners: int32 [512], replicated, may hold values from 0 to 31, as said below
Outputs:
- attended: bfloat16 [8192, 4096], P('ctx', 'tp')
Inputs may be any that keep to these rules, and one draw needn't show every extreme that they name: The 16 blocks of one index of ctx (blocks i * 16 to (i + 1) * 16 - 1) go to 16 different owners; for each position j < 16, the blocks i * 16 + j of all indices i go to all different owners, so every owner receives exactly one block of each position.
All inputs are finite; a program needn't handle non-finite values.
Results may differ from a plain program's by a relative error of at most 0.0055.
The roundings to bfloat16 on the way count: a program that leaves them out, or rounds other values in their place, can miss the bound.
Values may be sent and summed in bfloat16 or wider, within the bound.
A program may use at most 128 MiB of HBM per device.

v0:
```python
import math

import jax
import jax.numpy as jnp
from jax import lax
from jax.sharding import PartitionSpec as P

NEG_FILL = -1e30


def token_places(block_order, first_row, row_count, block_len):
    row_index = first_row + jnp.arange(row_count, dtype=jnp.int32)
    return block_order[row_index // block_len] * block_len + row_index % block_len


def documents(token_place, doc_ends):
    return jnp.sum((doc_ends[None, :] <= token_place[:, None]).astype(jnp.int32), axis=1)


def body(tokens, query_weight, keyval_weight, doc_lengths, owners):
    cycle_count = lax.axis_size("ctx")
    device = lax.axis_index("ctx")
    group_count = lax.axis_size("tp")
    share_rows = tokens.shape[0]
    tok_rows = share_rows * group_count
    per_device = owners.shape[0] // cycle_count
    block_len = tok_rows // per_device
    head_dim = keyval_weight.shape[1] // 2
    query_cols = query_weight.shape[1]
    block_order = jnp.argsort(owners, stable=True)
    doc_ends = jnp.cumsum(doc_lengths)
    owner_grid = owners.reshape(cycle_count, per_device)
    own_targets = lax.dynamic_index_in_dim(owner_grid, device, 0, keepdims=False)
    piece = lax.all_gather(tokens, "tp", axis=0, tiled=True)
    query_part = jnp.dot(piece, query_weight, preferred_element_type=jnp.float32).astype(
        jnp.bfloat16
    )
    keyval_part = jnp.dot(piece, keyval_weight, preferred_element_type=jnp.float32).astype(
        jnp.bfloat16
    )
    projected = jnp.concatenate([query_part, keyval_part], axis=1)
    columns = projected.shape[1]
    blocks = projected.reshape(own_targets.shape[0], block_len, columns)
    arrived = lax.all_to_all(
        jnp.zeros((cycle_count, block_len, columns), projected.dtype).at[own_targets].set(blocks),
        "ctx",
        split_axis=0,
        concat_axis=0,
        tiled=True,
    )
    sources = jnp.nonzero(owners == device, size=per_device)[0] // per_device
    projected = arrived[sources].reshape(tok_rows, arrived.shape[2])
    queries = projected[:, :query_cols]
    keyvals = projected[:, query_cols:]
    heads_here = query_cols // head_dim
    score_scale = 1.0 / math.sqrt(head_dim)
    query_heads = queries.reshape(tok_rows, heads_here, head_dim).transpose(1, 0, 2)
    query_place = token_places(block_order, device * tok_rows, tok_rows, block_len)
    query_docs = documents(query_place, doc_ends)
    initial = (
        jnp.full((heads_here, tok_rows), NEG_FILL, jnp.float32),
        jnp.zeros((heads_here, tok_rows), jnp.float32),
        jnp.zeros((heads_here, tok_rows, head_dim), jnp.float32),
    )
    key_piece = lax.all_gather(keyvals, "ctx", axis=0, tiled=True)
    count_rows = key_piece.shape[0]
    sub_rows = math.gcd(count_rows, 512)
    key_place = token_places(block_order, jnp.int32(0), count_rows, block_len)
    key_docs = documents(key_place, doc_ends)
    stacked = (
        key_piece.reshape(count_rows // sub_rows, sub_rows, key_piece.shape[1]),
        key_place.reshape(count_rows // sub_rows, sub_rows),
        key_docs.reshape(count_rows // sub_rows, sub_rows),
    )

    def advance(partial_value, member):
        keyval, member_place, member_docs = member
        allowed = (member_docs[None, :] == query_docs[:, None]) & (
            member_place[None, :] <= query_place[:, None]
        )

        def update(current):
            run_max, run_sum, run_acc = current
            scores = (
                jnp.einsum(
                    "hqd,kd->hqk",
                    query_heads,
                    keyval[:, :head_dim],
                    preferred_element_type=jnp.float32,
                )
                * score_scale
            )
            scores = jnp.where(allowed[None], scores, NEG_FILL)
            new_max = jnp.maximum(run_max, jnp.max(scores, axis=2))
            weights = jnp.where(allowed[None], jnp.exp(scores - new_max[:, :, None]), 0.0)
            factor = jnp.exp(run_max - new_max)
            new_sum = run_sum * factor + jnp.sum(weights, axis=2)
            new_acc = run_acc * factor[:, :, None] + jnp.einsum(
                "hqk,kd->hqd",
                weights.astype(jnp.bfloat16),
                keyval[:, head_dim:],
                preferred_element_type=jnp.float32,
            )
            return (new_max, new_sum, new_acc)

        def unchanged(current):
            return current

        return (lax.cond(jnp.any(allowed), update, unchanged, partial_value), None)

    finished, unused = lax.scan(advance, initial, stacked)
    attended = finished[2] / finished[1][:, :, None]
    return attended.transpose(1, 0, 2).reshape(tok_rows, heads_here * head_dim).astype(jnp.bfloat16)


def solution(mesh):
    return jax.shard_map(
        body,
        mesh=mesh,
        in_specs=(P(("ctx", "tp"), None), P(None, "tp"), P(None, "tp"), P(), P()),
        out_specs=P("ctx", "tp"),
        check_vma=False,
    )
```

profile of v0, /device:TPU:1, one launch (start us, length us, event | category | flops | bytes accessed | tf_op | source)
XLA Modules:
  0.0 275.2 jit_solution(502739521675465678)
XLA Ops:
  8.2 59.6 %all-gather.3.cloned.1.call-done = bf16[256,8192]{1,0:T(8,128)(2,1)} async-done(((bf16[32,8192]{1,0:T(8,128)(2,1)}), bf16[256,8192]{1,0:T(8,128)(2,1)}) %all-gather.3.cloned.1.call-update) | async-done | bytes 4194320 | tf_op jit(solution)/shard_map/all_gather | solution.py:34
  67.8 7.1 %convolution_convert_fusion = bf16[256,512]{1,0:T(8,128)(2,1)S(1)} fusion(bf16[256,8192]{1,0:T(8,128)(2,1)} %all-gather.3.cloned.1.call-done, bf16[8192,512]{1,0:T(8,128)(2,1)} %param.10), kind=kOutput, calls=%fused_computation.28 | convolution fusion | flops 2147614720 | bytes 12845056 | tf_op jit(solution)/shard_map/dot_general | solution.py:35
  75.0 1.2 convolution_convert_fusion.1
  76.3 0.9 broadcast_in_dim.60
  77.2 2.5 scatter_fusion
  79.7 10.1 %all-to-all-start = ((bf16[32,16,768]{2,1,0:T(8,128)(2,1)}), bf16[32,16,768]{2,1,0:T(8,128)(2,1)S(1)}, u32[]{:S(2)}, u32[]{:S(2)}) async-start(bf16[32,16,768]{2,1,0:T(8,128)(2,1)} %scatter_fusion), calls=%async_computation | async-start | bytes 1572864 | tf_op jit(solution)/shard_map/all_to_all | solution.py:44
  91.2 4.1 %scatter_custom_fusion.1 = s32[16]{0:T(128)S(1)} fusion(s32[512]{0:T(512)S(1)} %bitcast.63, s32[512]{0:T(512)S(1)} %broadcast.398, s32[]{:T(128)} %copy.68), kind=kCustom, calls=%fused_computation.89 | custom fusion | flops 512 | bytes 68 | tf_op jit(solution)/shard_map/scatter-add | solution.py:51
  96.2 16.5 %all-to-all-done = bf16[32,16,768]{2,1,0:T(8,128)(2,1)S(1)} async-done(((bf16[32,16,768]{2,1,0:T(8,128)(2,1)}), bf16[32,16,768]{2,1,0:T(8,128)(2,1)S(1)}, u32[]{:S(2)}, u32[]{:S(2)}) %all-to-all-start) | async-done | bytes 786464 | tf_op jit(solution)/shard_map/all_to_all | solution.py:44
  114.3 3.8 %sort.17 = (s32[512]{0:T(512)}, s32[512]{0:T(512)S(1)}) sort(s32[512]{0:T(512)S(1)} %copy-done, s32[512]{0:T(512)S(1)} %iota.37), dimensions={0}, to_apply=%region_6.7 | sort | flops 4608 | bytes 8192 | tf_op jit(solution)/shard_map/jit(argsort)/sort | solution.py:30
  118.1 1.9 gather_fusion.1
  120.1 51.2 %gather_fusion = s32[8192]{0:T(1024)S(1)} fusion(s32[512]{0:T(512)S(1)} %get-tuple-element.106, s32[8192]{0:T(1024)S(1)} %broadcast_clamp_fusion), kind=kCustom, calls=%fused_computation | custom fusion | bytes 98304 | tf_op jit(solution)/shard_map/gather | solution.py:13
  172.2 23.5 %all-gather.5.cloned.1.call-done = bf16[8192,256]{1,0:T(8,128)(2,1)} async-done(((bf16[256,256]{1,0:T(8,128)(2,1)}), bf16[8192,256]{1,0:T(8,128)(2,1)}) %all-gather.5.cloned.1.call-update) | async-done | bytes 4194320 | tf_op jit(solution)/shard_map/all_gather | solution.py:65
  195.7 71.7 %while.14 = (s32[]{:T(128)}, f32[4,256]{1,0:T(4,128)S(1)}, f32[4,256]{1,0:T(4,128)S(1)}, f32[4,256,128]{2,1,0:T(8,128)S(1)}, s32[16,512]{1,0:T(8,128)S(1)}, /*in...) while((s32[]{:T(128)}, f32[4,256]{1,0:T(4,128)S(1)}, ...), condition=%wide.region_16.17_spmd, body=%wide.region_10.16_spmd.sunk | while | flops 276039680 | bytes 8993003 | solution.py:111
  197.2 2.9 %conditional.2 = ((f32[4,256]{1,0:T(4,128)S(1)}, f32[4,256]{1,0:T(4,128)S(1)}, f32[4,256,128]{2,1,0:T(8,128)S(1)})) conditional(s32[]{:T(128)} %convert_element_type.54, (f32[4,256]{1,0:T(4,128)S(1)}, f32[4,256]{1,0:T(4,128)S(1)}, f32[4,256,128]{2,1,0:T(8,128)S(1)}) %tuple.42, (pred[256,512]{0,1:T(8,128)(4,1)S(1)}, ...), branch_computations={%region_12.12_spmd, %region_13.15_spmd} | conditional | flops 275515392 | bytes 8847396 | solution.py:109
  197.3 1.0 dynamic-slice_bitcast_fusion
  199.3 0.9 convolution_add_fusion
  201.7 2.9 %conditional.2 = ((f32[4,256]{1,0:T(4,128)S(1)}, f32[4,256]{1,0:T(4,128)S(1)}, f32[4,256,128]{2,1,0:T(8,128)S(1)})) conditional(s32[]{:T(128)} %convert_element_type.54, (f32[4,256]{1,0:T(4,128)S(1)}, f32[4,256]{1,0:T(4,128)S(1)}, f32[4,256,128]{2,1,0:T(8,128)S(1)}) %tuple.42, (pred[256,512]{0,1:T(8,128)(4,1)S(1)}, ...), branch_computations={%region_12.12_spmd, %region_13.15_spmd} | conditional | flops 275515392 | bytes 8847396 | solution.py:109
  201.7 1.0 dynamic-slice_bitcast_fusion
  203.8 0.9 convolution_add_fusion
  206.2 2.9 %conditional.2 = ((f32[4,256]{1,0:T(4,128)S(1)}, f32[4,256]{1,0:T(4,128)S(1)}, f32[4,256,128]{2,1,0:T(8,128)S(1)})) conditional(s32[]{:T(128)} %convert_element_type.54, (f32[4,256]{1,0:T(4,128)S(1)}, f32[4,256]{1,0:T(4,128)S(1)}, f32[4,256,128]{2,1,0:T(8,128)S(1)}) %tuple.42, (pred[256,512]{0,1:T(8,128)(4,1)S(1)}, ...), branch_computations={%region_12.12_spmd, %region_13.15_spmd} | conditional | flops 275515392 | bytes 8847396 | solution.py:109
  206.2 1.0 dynamic-slice_bitcast_fusion
  210.7 2.9 %conditional.2 = ((f32[4,256]{1,0:T(4,128)S(1)}, f32[4,256]{1,0:T(4,128)S(1)}, f32[4,256,128]{2,1,0:T(8,128)S(1)})) conditional(s32[]{:T(128)} %convert_element_type.54, (f32[4,256]{1,0:T(4,128)S(1)}, f32[4,256]{1,0:T(4,128)S(1)}, f32[4,256,128]{2,1,0:T(8,128)S(1)}) %tuple.42, (pred[256,512]{0,1:T(8,128)(4,1)S(1)}, ...), branch_computations={%region_12.12_spmd, %region_13.15_spmd} | conditional | flops 275515392 | bytes 8847396 | solution.py:109
  210.7 1.0 dynamic-slice_bitcast_fusion
  215.2 2.9 %conditional.2 = ((f32[4,256]{1,0:T(4,128)S(1)}, f32[4,256]{1,0:T(4,128)S(1)}, f32[4,256,128]{2,1,0:T(8,128)S(1)})) conditional(s32[]{:T(128)} %convert_element_type.54, (f32[4,256]{1,0:T(4,128)S(1)}, f32[4,256]{1,0:T(4,128)S(1)}, f32[4,256,128]{2,1,0:T(8,128)S(1)}) %tuple.42, (pred[256,512]{0,1:T(8,128)(4,1)S(1)}, ...), branch_computations={%region_12.12_spmd, %region_13.15_spmd} | conditional | flops 275515392 | bytes 8847396 | solution.py:109
  215.2 1.0 dynamic-slice_bitcast_fusion
  219.6 2.9 %conditional.2 = ((f32[4,256]{1,0:T(4,128)S(1)}, f32[4,256]{1,0:T(4,128)S(1)}, f32[4,256,128]{2,1,0:T(8,128)S(1)})) conditional(s32[]{:T(128)} %convert_element_type.54, (f32[4,256]{1,0:T(4,128)S(1)}, f32[4,256]{1,0:T(4,128)S(1)}, f32[4,256,128]{2,1,0:T(8,128)S(1)}) %tuple.42, (pred[256,512]{0,1:T(8,128)(4,1)S(1)}, ...), branch_computations={%region_12.12_spmd, %region_13.15_spmd} | conditional | flops 275515392 | bytes 8847396 | solution.py:109
  219.7 1.0 dynamic-slice_bitcast_fusion
  224.1 2.9 %conditional.2 = ((f32[4,256]{1,0:T(4,128)S(1)}, f32[4,256]{1,0:T(4,128)S(1)}, f32[4,256,128]{2,1,0:T(8,128)S(1)})) conditional(s32[]{:T(128)} %convert_element_type.54, (f32[4,256]{1,0:T(4,128)S(1)}, f32[4,256]{1,0:T(4,128)S(1)}, f32[4,256,128]{2,1,0:T(8,128)S(1)}) %tuple.42, (pred[256,512]{0,1:T(8,128)(4,1)S(1)}, ...), branch_computations={%region_12.12_spmd, %region_13.15_spmd} | conditional | flops 275515392 | bytes 8847396 | solution.py:109
  224.1 1.0 dynamic-slice_bitcast_fusion
  228.6 2.9 %conditional.2 = ((f32[4,256]{1,0:T(4,128)S(1)}, f32[4,256]{1,0:T(4,128)S(1)}, f32[4,256,128]{2,1,0:T(8,128)S(1)})) conditional(s32[]{:T(128)} %convert_element_type.54, (f32[4,256]{1,0:T(4,128)S(1)}, f32[4,256]{1,0:T(4,128)S(1)}, f32[4,256,128]{2,1,0:T(8,128)S(1)}) %tuple.42, (pred[256,512]{0,1:T(8,128)(4,1)S(1)}, ...), branch_computations={%region_12.12_spmd, %region_13.15_spmd} | conditional | flops 275515392 | bytes 8847396 | solution.py:109
  228.6 1.0 dynamic-slice_bitcast_fusion
  233.1 2.9 %conditional.2 = ((f32[4,256]{1,0:T(4,128)S(1)}, f32[4,256]{1,0:T(4,128)S(1)}, f32[4,256,128]{2,1,0:T(8,128)S(1)})) conditional(s32[]{:T(128)} %convert_element_type.54, (f32[4,256]{1,0:T(4,128)S(1)}, f32[4,256]{1,0:T(4,128)S(1)}, f32[4,256,128]{2,1,0:T(8,128)S(1)}) %tuple.42, (pred[256,512]{0,1:T(8,128)(4,1)S(1)}, ...), branch_computations={%region_12.12_spmd, %region_13.15_spmd} | conditional | flops 275515392 | bytes 8847396 | solution.py:109
  233.1 1.0 dynamic-slice_bitcast_fusion
  237.6 2.9 %conditional.2 = ((f32[4,256]{1,0:T(4,128)S(1)}, f32[4,256]{1,0:T(4,128)S(1)}, f32[4,256,128]{2,1,0:T(8,128)S(1)})) conditional(s32[]{:T(128)} %convert_element_type.54, (f32[4,256]{1,0:T(4,128)S(1)}, f32[4,256]{1,0:T(4,128)S(1)}, f32[4,256,128]{2,1,0:T(8,128)S(1)}) %tuple.42, (pred[256,512]{0,1:T(8,128)(4,1)S(1)}, ...), branch_computations={%region_12.12_spmd, %region_13.15_spmd} | conditional | flops 275515392 | bytes 8847396 | solution.py:109
  237.6 1.0 dynamic-slice_bitcast_fusion
  242.0 2.9 %conditional.2 = ((f32[4,256]{1,0:T(4,128)S(1)}, f32[4,256]{1,0:T(4,128)S(1)}, f32[4,256,128]{2,1,0:T(8,128)S(1)})) conditional(s32[]{:T(128)} %convert_element_type.54, (f32[4,256]{1,0:T(4,128)S(1)}, f32[4,256]{1,0:T(4,128)S(1)}, f32[4,256,128]{2,1,0:T(8,128)S(1)}) %tuple.42, (pred[256,512]{0,1:T(8,128)(4,1)S(1)}, ...), branch_computations={%region_12.12_spmd, %region_13.15_spmd} | conditional | flops 275515392 | bytes 8847396 | solution.py:109
  242.1 1.0 dynamic-slice_bitcast_fusion
  246.5 2.9 %conditional.2 = ((f32[4,256]{1,0:T(4,128)S(1)}, f32[4,256]{1,0:T(4,128)S(1)}, f32[4,256,128]{2,1,0:T(8,128)S(1)})) conditional(s32[]{:T(128)} %convert_element_type.54, (f32[4,256]{1,0:T(4,128)S(1)}, f32[4,256]{1,0:T(4,128)S(1)}, f32[4,256,128]{2,1,0:T(8,128)S(1)}) %tuple.42, (pred[256,512]{0,1:T(8,128)(4,1)S(1)}, ...), branch_computations={%region_12.12_spmd, %region_13.15_spmd} | conditional | flops 275515392 | bytes 8847396 | solution.py:109
  246.5 1.0 dynamic-slice_bitcast_fusion
  251.0 2.9 %conditional.2 = ((f32[4,256]{1,0:T(4,128)S(1)}, f32[4,256]{1,0:T(4,128)S(1)}, f32[4,256,128]{2,1,0:T(8,128)S(1)})) conditional(s32[]{:T(128)} %convert_element_type.54, (f32[4,256]{1,0:T(4,128)S(1)}, f32[4,256]{1,0:T(4,128)S(1)}, f32[4,256,128]{2,1,0:T(8,128)S(1)}) %tuple.42, (pred[256,512]{0,1:T(8,128)(4,1)S(1)}, ...), branch_computations={%region_12.12_spmd, %region_13.15_spmd} | conditional | flops 275515392 | bytes 8847396 | solution.py:109
  251.0 1.0 dynamic-slice_bitcast_fusion
  255.5 2.9 %conditional.2 = ((f32[4,256]{1,0:T(4,128)S(1)}, f32[4,256]{1,0:T(4,128)S(1)}, f32[4,256,128]{2,1,0:T(8,128)S(1)})) conditional(s32[]{:T(128)} %convert_element_type.54, (f32[4,256]{1,0:T(4,128)S(1)}, f32[4,256]{1,0:T(4,128)S(1)}, f32[4,256,128]{2,1,0:T(8,128)S(1)}) %tuple.42, (pred[256,512]{0,1:T(8,128)(4,1)S(1)}, ...), branch_computations={%region_12.12_spmd, %region_13.15_spmd} | conditional | flops 275515392 | bytes 8847396 | solution.py:109
  255.5 1.0 dynamic-slice_bitcast_fusion
  260.0 2.9 %conditional.2 = ((f32[4,256]{1,0:T(4,128)S(1)}, f32[4,256]{1,0:T(4,128)S(1)}, f32[4,256,128]{2,1,0:T(8,128)S(1)})) conditional(s32[]{:T(128)} %convert_element_type.54, (f32[4,256]{1,0:T(4,128)S(1)}, f32[4,256]{1,0:T(4,128)S(1)}, f32[4,256,128]{2,1,0:T(8,128)S(1)}) %tuple.42, (pred[256,512]{0,1:T(8,128)(4,1)S(1)}, ...), branch_computations={%region_12.12_spmd, %region_13.15_spmd} | conditional | flops 275515392 | bytes 8847396 | solution.py:109
  260.0 1.0 dynamic-slice_bitcast_fusion
  264.4 2.9 %conditional.2 = ((f32[4,256]{1,0:T(4,128)S(1)}, f32[4,256]{1,0:T(4,128)S(1)}, f32[4,256,128]{2,1,0:T(8,128)S(1)})) conditional(s32[]{:T(128)} %convert_element_type.54, (f32[4,256]{1,0:T(4,128)S(1)}, f32[4,256]{1,0:T(4,128)S(1)}, f32[4,256,128]{2,1,0:T(8,128)S(1)}) %tuple.42, (pred[256,512]{0,1:T(8,128)(4,1)S(1)}, ...), branch_computations={%region_12.12_spmd, %region_13.15_spmd} | conditional | flops 275515392 | bytes 8847396 | solution.py:109
  264.5 1.0 dynamic-slice_bitcast_fusion
  267.4 0.9 copy_bitcast_fusion
  (179 shorter events, 49.1 us)
Async XLA Ops:
  6.5 61.3 %all-gather.3.cloned.1.call-start = ((), (), s32[]{:S(2)}) async-start(), calls=%async_computation.1 | async-start | bytes 4718592 | tf_op jit(solution)/shard_map/all_gather | solution.py:34
  67.8 7.1 %copy-start.2 = (bf16[8192,256]{1,0:T(8,128)(2,1)S(1)}, bf16[8192,256]{1,0:T(8,128)(2,1)}, u32[]{:S(2)}) copy-start(bf16[8192,256]{1,0:T(8,128)(2,1)} %param.11) | copy-start | bytes 12582916
  67.8 7.1 %copy-start.3 = (bf16[256,8192]{1,0:T(8,128)(2,1)S(1)}, bf16[256,8192]{1,0:T(8,128)(2,1)}, u32[]{:S(2)}) copy-start(bf16[256,8192]{1,0:T(8,128)(2,1)} %all-gather.3.cloned.1.call-done) | copy-start | bytes 12582916
  76.2 13.7 %copy-start = (s32[512]{0:T(512)S(1)}, s32[512]{0:T(512)}, u32[]{:S(2)}) copy-start(s32[512]{0:T(512)} %param.13) | copy-start | bytes 6148
  77.2 36.7 %copy-start.1 = (s32[64]{0:T(128)S(1)}, s32[64]{0:T(128)}, u32[]{:S(2)}) copy-start(s32[64]{0:T(128)} %param.12) | copy-start | bytes 772
  79.7 32.9 %all-to-all-start = ((bf16[32,16,768]{2,1,0:T(8,128)(2,1)}), bf16[32,16,768]{2,1,0:T(8,128)(2,1)S(1)}, u32[]{:S(2)}, u32[]{:S(2)}) async-start(bf16[32,16,768]{2,1,0:T(8,128)(2,1)} %scatter_fusion), calls=%async_computation | async-start | bytes 1572864 | tf_op jit(solution)/shard_map/all_to_all | solution.py:44
  89.9 105.8 %all-gather.5.cloned.1.call-start = ((), (), s32[]{:S(2)}) async-start(), calls=%async_computation.2 | async-start | bytes 4325376 | tf_op jit(solution)/shard_map/all_gather | solution.py:65
Sparse Core Ops, SparseCore 0:
  9.1 58.6 all-gather.2
  114.0 81.5 all-gather.4
where the time goes:
time: 276 us; the launch traced here: 275 us
  waiting for transfers between devices  100 us (36%)
  local copies, waits for them, and re-layouts  75.3 us (27%)
  other arithmetic  33.8 us (12%)
  matrix products  30.3 us (11%)
  between operations  13.6 us (5%)
  loops' own time  11.6 us (4%)
  starting transfers between devices  10.2 us (4%)
    all_gather x1, waiting for transfers between devices, body(): piece = lax.all_gather(tokens, 'tp', axis=0, tiled=True)  59.6 us
    gather x2, local copies, waits for them, and re-layouts, token_places(): block_order[row_index // block_len] * block_len + row_index % block_len  53.2 us
    all_gather x1, waiting for transfers between devices, body(): key_piece = lax.all_gather(keyvals, 'ctx', axis=0, tiled=True)  23.5 us
    all_to_all x1, waiting for transfers between devices, body(): lax.all_to_all(jnp.zeros((cycle_count, block_len, columns), projected.dty...  16.5 us
    squeeze x16, local copies, waits for them, and re-layouts, body(): finished, unused = lax.scan(advance, initial, stacked)  15.6 us
    dot_general x16, matrix products, update(): jnp.einsum('hqk,kd->hqd', weights.astype(jnp.bfloat16), keyval[:, head_di...  13.9 us
    reduce_or x16, other arithmetic, advance(): return (lax.cond(jnp.any(allowed), update, unchanged, partial_value), None)  13.4 us
    another operation x1, loops' own time, body(): finished, unused = lax.scan(advance, initial, stacked)  10.9 us
  transfers between devices with their start and end apart: 3, of which 3 were waited for; matrix products, arithmetic and copies ran while one was open for 24% of the time, Pallas kernels for 0%

commit v1 on v0

v1 whole, which is shorter than its diff:
```python
import functools
import math

import jax
import jax.numpy as jnp
from jax import lax
from jax.experimental import pallas as pl
from jax.experimental.pallas import tpu as pltpu
from jax.sharding import PartitionSpec as P

NEG_FILL = -1e30
DOC_MOST = 2048
MESH = pl.DeviceIdType.MESH
PIECES = 4
X_FIRST = (0, 1)
Y_FIRST = (2, 3)
GO_RIGHT = (0, 2)
GO_LEFT = (1, 3)
HEAD_CHUNK = 2


def gather_kernel(cfg, tok_hbm, qw_hbm, kw_hbm, qbuf, kv_out,
                  tok, wq, wk, kvwin, load_sem, w_sem, tsend, trecv, ksend, krecv):
    n_ctx, n_x, reach, rows, share, depth, heads, hd, blk, n_docs = cfg
    me = lax.axis_index("ctx")
    g = lax.axis_index("tp")
    y = g // n_x
    x = g % n_x
    core = me % 2
    xr = (x + 1) % n_x
    xl = (x + n_x - 1) % n_x
    xo = (x + 2) % n_x
    yo = 1 - y
    chunk_rows = 2 * share
    per_dev = rows // blk
    part = depth // PIECES

    def shard_rows(yy, xx):
        return pl.ds(pl.multiple_of((xx * 2 + yy) * share, share), share)

    def group(yy, xx):
        return yy * n_x + xx

    loads = []
    for p in range(PIECES):
        c = pltpu.make_async_copy(tok_hbm.at[:, pl.ds(p * part, part)],
                                  tok.at[p, shard_rows(y, x), :], load_sem.at[p])
        c.start()
        loads.append(c)
    wloads = []
    for p in range(PIECES):
        c = pltpu.make_async_copy(kw_hbm.at[pl.ds(p * part, part), :], wk.at[p], w_sem.at[p])
        c.start()
        wloads.append(c)
        c = pltpu.make_async_copy(qw_hbm.at[pl.ds(p * part, part), :], wq.at[p],
                                  w_sem.at[PIECES + p])
        c.start()
        wloads.append(c)

    barrier = pltpu.get_barrier_semaphore()
    for gg in (group(y, xr), group(y, xl), group(yo, x)):
        pl.semaphore_signal(barrier, inc=1, device_id={"tp": gg}, device_id_type=MESH)

    for cc in ((me + 2) % n_ctx, (me + n_ctx - 2) % n_ctx, me + 1 - 2 * core):
        pl.semaphore_signal(barrier, inc=1, device_id={"ctx": cc}, device_id_type=MESH)
    pl.semaphore_wait(barrier, 6)
    for c in loads:
        c.wait()

    sent = []

    def tok_copy(gg, yy, xx, p, sem):
        where = tok.at[p, shard_rows(yy, xx), :]
        return pltpu.make_async_remote_copy(
            src_ref=where, dst_ref=where, send_sem=tsend.at[sem],
            recv_sem=trecv.at[(xx * 2 + yy) * PIECES + p],
            device_id={"tp": gg}, device_id_type=MESH)

    def send(gg, yy, xx, p):
        c = tok_copy(gg, yy, xx, p, len(sent))
        c.start()
        sent.append(c)

    def got(yy, xx, p):
        tok_copy(g, yy, xx, p, 0).wait_recv()

    right, left, over = group(y, xr), group(y, xl), group(yo, x)
    for p in Y_FIRST + X_FIRST:
        send(over, y, x, p)
    for p in X_FIRST + Y_FIRST:
        send(right, y, x, p)
        send(left, y, x, p)

    ksent = []
    chunk_x = (x, xl, xr, xo)

    def chunk_at(k):
        return pl.ds(pl.multiple_of(chunk_x[k] * chunk_rows, chunk_rows), chunk_rows)

    def kv_copy(target, src_slot, dst_slot, k, sem):
        return pltpu.make_async_remote_copy(
            src_ref=kvwin.at[src_slot, chunk_at(k), :],
            dst_ref=kvwin.at[dst_slot, chunk_at(k), :],
            send_sem=ksend.at[sem], recv_sem=krecv.at[dst_slot * 4 + k],
            device_id={"ctx": target}, device_id_type=MESH)

    def kv_send(target, src_slot, dst_slot, k):
        c = kv_copy(target, src_slot, dst_slot, k, len(ksent))
        c.start()
        ksent.append(c)

    def kv_got(slot, k):
        kv_copy(me, slot, slot, k, 0).wait_recv()

    up = (me + 2) % n_ctx
    twin = me + 1 - 2 * core

    def kv_step(step):
        for d in range(0, reach + 1):
            k = step - d
            if k < 0 or k > 3:
                continue
            slot = d * 2 + core
            if d > 0:
                kv_got(slot, k)
            if d < reach:
                kv_send(up, slot, slot + 2, k)
            kv_send(twin, slot, slot, k)

    def project(k):
        at = chunk_at(k)

        def kv_part(p, acc):
            return acc + jnp.dot(tok[p, at, :], wk[p], preferred_element_type=jnp.float32)

        kv = lax.fori_loop(0, PIECES, kv_part, jnp.zeros((chunk_rows, 2 * hd), jnp.float32))
        kvwin[core, at, :] = kv.astype(jnp.bfloat16)
        kv_step(k)

        def q_part(p, acc):
            return acc + jnp.dot(tok[p, at, :], wq[p], preferred_element_type=jnp.float32)

        q = lax.fori_loop(0, PIECES, q_part, jnp.zeros((chunk_rows, heads * hd), jnp.float32))
        q = q.astype(jnp.bfloat16)
        for h in range(heads):
            qbuf[h, at, :] = q[:, h * hd:(h + 1) * hd]

    for p in Y_FIRST:
        got(yo, x, p)
        send(right, yo, x, p)
        send(left, yo, x, p)
    for p in X_FIRST:
        got(y, xl, p)
        if p in GO_RIGHT:
            send(right, y, xl, p)
        send(over, y, xl, p)
        got(y, xr, p)
        if p in GO_LEFT:
            send(left, y, xr, p)
        send(over, y, xr, p)
    for c in wloads:
        c.wait()
    for p in X_FIRST:
        got(yo, x, p)
    project(0)
    for p in Y_FIRST:
        got(y, xl, p)
        if p in GO_RIGHT:
            send(right, y, xl, p)
        got(y, xr, p)
        if p in GO_LEFT:
            send(left, y, xr, p)
    for p in X_FIRST:
        got(y, xo, p)
        send(over, y, xo, p)
    for p in Y_FIRST:
        got(yo, xl, p)
        if p in GO_RIGHT:
            send(right, yo, xl, p)
        got(yo, xr, p)
        if p in GO_LEFT:
            send(left, yo, xr, p)
    for p in X_FIRST:
        got(yo, xl, p)
    project(1)
    for p in X_FIRST:
        got(yo, xr, p)
    project(2)
    for p in Y_FIRST:
        got(y, xo, p)
    for p in X_FIRST:
        got(yo, xo, p)
    for p in Y_FIRST:
        got(yo, xo, p)
    project(3)

    for m in range(1, reach + 1):
        kv_step(3 + m)
    for d in range(reach + 1):
        for k in range(4):
            kv_got(d * 2 + 1 - core, k)
    kv_out[...] = kvwin[...]
    for c in sent:
        c.wait_send()
    for c in ksent:
        c.wait_send()


def attend_kernel(cfg, qbuf, kvwin, doc_ref, own_ref, out_ref,
                  sbuf, mbuf, obuf, sendbuf, recvbuf, pmat, rmat, asend, arecv):
    n_ctx, n_x, reach, rows, share, depth, heads, hd, blk, n_docs = cfg
    me = lax.axis_index("ctx")
    core = me % 2
    chunk_rows = 2 * share
    per_dev = rows // blk
    barrier = pltpu.get_barrier_semaphore()

    def greet(d, carry):
        pl.semaphore_signal(barrier, inc=1, device_id={"ctx": (me + d) % n_ctx},
                            device_id_type=MESH)
        return carry

    lax.fori_loop(1, n_ctx, greet, 0)

    def place(index):
        return ((index // share) % 2) * (n_x * share) + (index // chunk_rows) * share + index % share

    row_place = me * rows + place(lax.broadcasted_iota(jnp.int32, (rows, 1), 0))

    def next_doc(d, carry):
        end, start = carry
        end = end + doc_ref[d]
        return end, jnp.where(row_place >= end, end, start)

    row_start = lax.fori_loop(0, n_docs, next_doc,
                              (jnp.int32(0), jnp.zeros((rows, 1), jnp.int32)))[1]

    lane_place = place(lax.broadcasted_iota(jnp.int32, (1, rows), 1))

    def block_owner(j, carry):
        return jnp.where(lane_place // blk == j, own_ref[me * per_dev + j], carry)

    lane_owner = lax.fori_loop(0, per_dev, block_owner, jnp.zeros((1, rows), jnp.int32))
    slot_row = lax.broadcasted_iota(jnp.int32, (n_ctx * blk, 1), 0)
    pmat[...] = jnp.where(
        (slot_row // blk == lane_owner) & (slot_row % blk == lane_place % blk), 1.0, 0.0
    ).astype(jnp.bfloat16)
    slot_lane = lax.broadcasted_iota(jnp.int32, (1, n_ctx * blk), 1)

    def source(s, carry):
        count, rank = carry
        hit = jnp.int32(0)
        for j in range(per_dev):
            hit = hit + jnp.where(own_ref[s * per_dev + j] == me, 1, 0)
        mine = (slot_lane // blk == s) & (jnp.full(slot_lane.shape, hit, jnp.int32) > 0)
        return count + hit, jnp.where(mine, count, rank)

    rank = lax.fori_loop(0, n_ctx, source,
                         (jnp.int32(0), jnp.full((1, n_ctx * blk), -1, jnp.int32)))[1]
    out_row = lax.broadcasted_iota(jnp.int32, (rows, 1), 0)
    rmat[...] = jnp.where(
        (out_row // blk == rank) & (out_row % blk == slot_lane % blk), 1.0, 0.0
    ).astype(jnp.bfloat16)

    mbuf[...] = jnp.full(mbuf.shape, NEG_FILL, jnp.float32)

    def window_slot(t):
        return ((t - core + 1) // 2) * 2 + (core + t) % 2

    def score(t):
        slot = window_slot(t)
        key_place = ((me + n_ctx - t) % n_ctx) * rows + lane_place
        allowed = (key_place >= row_start) & (key_place <= row_place)

        def one(h, carry):
            s = lax.dot_general(qbuf[h], kvwin[slot, :, 0:hd], (((1,), (1,)), ((), ())),
                                preferred_element_type=jnp.float32)
            s = jnp.where(allowed, s, NEG_FILL)
            sbuf[h, t] = s
            m = mbuf[h]
            for c in range(rows // 128):
                m = jnp.maximum(m, s[:, c * 128:(c + 1) * 128])
            mbuf[h] = m
            return carry

        lax.fori_loop(0, heads, one, 0)

    for t in range(2 * reach + 1):
        score(t)

    scale = math.log2(math.e) / math.sqrt(hd)
    half = rows // 2
    asent = []

    def finish(h, column):
        for r in range(2):
            at = pl.ds(r * half, half)
            top = jnp.max(mbuf[h, at, :], axis=1, keepdims=True)

            def step(t, carry):
                total, acc = carry
                w = jnp.exp2((sbuf[h, t, at, :] - top) * scale)
                for c in range(rows // 128):
                    total = total + w[:, c * 128:(c + 1) * 128]
                acc = acc + jnp.dot(w.astype(jnp.bfloat16), kvwin[window_slot(t), :, hd:2 * hd],
                                    preferred_element_type=jnp.float32)
                return total, acc

            total, acc = lax.fori_loop(0, 2 * reach + 1, step,
                                       (jnp.zeros((half, 128), jnp.float32),
                                        jnp.zeros((half, hd), jnp.float32)))
            value = acc / jnp.sum(total, axis=1, keepdims=True)
            obuf[at, column * hd:(column + 1) * hd] = value.astype(jnp.bfloat16)

    wide = HEAD_CHUNK * hd

    def a_copy(chunk, d):
        target = (me + d) % n_ctx
        return pltpu.make_async_remote_copy(
            src_ref=sendbuf.at[chunk, pl.ds(pl.multiple_of(target * blk, blk), blk), :],
            dst_ref=recvbuf.at[chunk, pl.ds(pl.multiple_of(me * blk, blk), blk), :],
            send_sem=asend.at[chunk * n_ctx + d], recv_sem=arecv.at[chunk * n_ctx + d],
            device_id={"ctx": target}, device_id_type=MESH)

    def a_got(chunk, d):
        source = (me + n_ctx - d) % n_ctx
        where = recvbuf.at[chunk, pl.ds(pl.multiple_of(source * blk, blk), blk), :]
        pltpu.make_async_remote_copy(
            src_ref=where, dst_ref=where,
            send_sem=asend.at[chunk * n_ctx + d], recv_sem=arecv.at[chunk * n_ctx + d],
            device_id={"ctx": source}, device_id_type=MESH).wait_recv()

    pl.semaphore_wait(barrier, n_ctx - 1)
    chunks = heads // HEAD_CHUNK
    my_slot = pl.ds(pl.multiple_of(me * blk, blk), blk)
    for chunk in range(chunks):
        for c in range(HEAD_CHUNK):
            finish(chunk * HEAD_CHUNK + c, c)
        sendbuf[chunk] = jnp.dot(pmat[...], obuf[...],
                                 preferred_element_type=jnp.float32).astype(jnp.bfloat16)

        def go(d, carry):
            a_copy(chunk, d).start()
            return carry

        lax.fori_loop(1, n_ctx, go, 0)
        recvbuf[chunk, my_slot, :] = sendbuf[chunk, my_slot, :]

    for chunk in range(chunks):
        def arrived(d, carry):
            a_got(chunk, d)
            return carry

        lax.fori_loop(1, n_ctx, arrived, 0)
        out_ref[:, chunk * wide:(chunk + 1) * wide] = jnp.dot(
            rmat[...], recvbuf[chunk], preferred_element_type=jnp.float32).astype(jnp.bfloat16)

    for chunk in range(chunks):
        def gone(d, carry):
            a_copy(chunk, d).wait_send()
            return carry

        lax.fori_loop(1, n_ctx, gone, 0)


def body(tokens, query_weight, keyval_weight, doc_lengths, owners):
    n_ctx = lax.axis_size("ctx")
    n_tp = lax.axis_size("tp")
    n_x = n_tp // 2
    share, depth = tokens.shape
    rows = share * n_tp
    hd = keyval_weight.shape[1] // 2
    heads = query_weight.shape[1] // hd
    per_dev = owners.shape[0] // n_ctx
    blk = rows // per_dev
    reach = -(-DOC_MOST // (2 * rows))
    n_docs = doc_lengths.shape[0]
    cfg = (n_ctx, n_x, reach, rows, share, depth, heads, hd, blk, n_docs)
    part = depth // PIECES
    slots = 2 * (reach + 1)
    chunks = heads // HEAD_CHUNK
    wide = HEAD_CHUNK * hd
    bf, f32 = jnp.bfloat16, jnp.float32
    n_tok = 12 + 4 * len(Y_FIRST) + 4 * len(X_FIRST) + 8
    n_kv = 4 * (2 * reach + 1)
    dma = pltpu.SemaphoreType.DMA
    q, kv = pl.pallas_call(
        functools.partial(gather_kernel, cfg),
        out_shape=(jax.ShapeDtypeStruct((heads, rows, hd), bf),
                   jax.ShapeDtypeStruct((slots, rows, 2 * hd), bf)),
        in_specs=[pl.BlockSpec(memory_space=pl.ANY)] * 3,
        out_specs=[pl.BlockSpec(memory_space=pltpu.VMEM)] * 2,
        scratch_shapes=[
            pltpu.VMEM((PIECES, rows, part), bf),
            pltpu.VMEM((PIECES, part, heads * hd), bf),
            pltpu.VMEM((PIECES, part, 2 * hd), bf),
            pltpu.VMEM((slots, rows, 2 * hd), bf),
            dma((PIECES,)),
            dma((2 * PIECES,)),
            dma((n_tok,)),
            dma((2 * n_x * PIECES,)),
            dma((n_kv,)),
            dma((slots * 4,)),
        ],
        compiler_params=pltpu.CompilerParams(
            collective_id=0, has_side_effects=True, vmem_limit_bytes=48 * 1024 * 1024
        ),
    )(tokens, query_weight, keyval_weight)
    return pl.pallas_call(
        functools.partial(attend_kernel, cfg),
        out_shape=jax.ShapeDtypeStruct((rows, heads * hd), bf),
        in_specs=[pl.BlockSpec(memory_space=pltpu.VMEM)] * 2
        + [pl.BlockSpec(memory_space=pltpu.SMEM)] * 2,
        out_specs=pl.BlockSpec(memory_space=pltpu.VMEM),
        scratch_shapes=[
            pltpu.VMEM((heads, 2 * reach + 1, rows, rows), f32),
            pltpu.VMEM((heads, rows, 128), f32),
            pltpu.VMEM((rows, wide), bf),
            pltpu.VMEM((chunks, n_ctx * blk, wide), bf),
            pltpu.VMEM((chunks, n_ctx * blk, wide), bf),
            pltpu.VMEM((n_ctx * blk, rows), bf),
            pltpu.VMEM((rows, n_ctx * blk), bf),
            dma((chunks * n_ctx,)),
            dma((chunks * n_ctx,)),
        ],
        compiler_params=pltpu.CompilerParams(
            collective_id=1, has_side_effects=True, vmem_limit_bytes=48 * 1024 * 1024
        ),
    )(q, kv, doc_lengths, owners)


def solution(mesh):
    return jax.shard_map(
        body,
        mesh=mesh,
        in_specs=(P(("ctx", "tp"), None), P(None, "tp"), P(None, "tp"), P(), P()),
        out_specs=P("ctx", "tp"),
        check_vma=False,
    )
```

time: 276 us -> 104 us (0.38)
  Pallas kernels: 0 us -> 103 us
  waiting for transfers between devices: 100 us -> 0 us
  local copies, waits for them, and re-layouts: 75.3 us -> 1.75 us
  other arithmetic: 33.8 us -> 0 us
  matrix products: 30.3 us -> 0 us
  between operations: 13.6 us -> 0.03 us
  loops' own time: 11.6 us -> 0 us
  starting transfers between devices: 10.2 us -> 0 us
    pallas_call x0 -> x2, Pallas kernels: none -> 103 us  [the longest x1 57.6 us: body(): pl.pallas_call(functools.partial(gather_kernel, cfg), out_shape=(jax.Shap...]
    all_gather x2 -> x0, waiting for transfers between devices: 83.1 us -> none  [the longest x1 59.6 us: body(): piece = lax.all_gather(tokens, 'tp', axis=0, tiled=True)]
    gather x3 -> x0, local copies, waits for them, and re-layouts: 53.7 us -> none  [the longest x2 53.2 us: token_places(): block_order[row_index // block_len] * block_len + row_index % block_len]
    dot_general x34 -> x0, matrix products: 30.3 us -> none  [the longest x16 13.9 us: update(): jnp.einsum('hqk,kd->hqd', weights.astype(jnp.bfloat16), keyval[:, head_di...]
    all_to_all x1 -> x0, waiting for transfers between devices: 16.5 us -> none  [body(): lax.all_to_all(jnp.zeros((cycle_count, block_len, columns), projected.dty...]
    squeeze x18 -> x0, local copies, waits for them, and re-layouts: 15.7 us -> none  [the longest x16 15.6 us: body(): finished, unused = lax.scan(advance, initial, stacked)]
    reduce_or x16 -> x0, other arithmetic: 13.4 us -> none  [advance(): return (lax.cond(jnp.any(allowed), update, unchanged, partial_value), None)]
    another operation x17 -> x0, loops' own time: 11.6 us -> none  [the longest x1 10.9 us: body(): finished, unused = lax.scan(advance, initial, stacked)]
  transfers between devices with their start and end apart: 3 -> 0, of which waited for: 3 -> 0; matrix products, arithmetic and copies ran while one was open for 24% -> 0% of each run, Pallas kernels for 0% -> 0%
where the time goes in v1:
time: 104 us
  Pallas kernels  103 us (99%)
  local copies, waits for them, and re-layouts  1.75 us (2%)
    pallas_call x1, Pallas kernels, body(): pl.pallas_call(functools.partial(gather_kernel, cfg), out_shape=(jax.Shap...  57.6 us
    pallas_call x1, Pallas kernels, body(): pl.pallas_call(functools.partial(attend_kernel, cfg), out_shape=jax.Shape...  44.9 us

profile of v1, /device:TPU:1, one launch (start us, length us, event | category | flops | bytes accessed | tf_op | source)
XLA Modules:
  0.0 104.4 jit_solution(8729769069228260867)
XLA Ops:
  0.0 0.0 copy-start
  0.0 1.0 copy-done
  1.0 0.0 copy-start.1
  1.0 0.0 copy-start.2
  1.0 57.6 %shard_map.55 = (bf16[4,256,128]{2,1,0:T(8,128)(2,1)S(1)}, bf16[10,256,256]{2,1,0:T(8,128)(2,1)S(1)}) custom-call(bf16[32,8192]{1,0:T(8,128)(2,1)S(1)} %copy-done, bf16[8192,512]{1,0:T(8,128)(2,1)} %qw_hbm.1, bf16[8192,256]{1,0:T(8,128)(2,1)} %kw_hbm.1), custom_call_target="tpu_custom_call" | custom-call | tf_op jit(solution)/shard_map/pallas_call | solution.py:387
  58.7 0.0 copy-done.1
  58.7 0.0 copy-done.2
  58.7 44.9 %shard_map.56 = bf16[256,512]{1,0:T(8,128)(2,1)S(1)} custom-call(bf16[4,256,128]{2,1,0:T(8,128)(2,1)S(1)} %get-tuple-element.7.qbuf, bf16[10,256,256]{2,1,0:T(8,128)(2,1)S(1)} %get-tuple-element.8.kvwin, s32[64]{0:T(128)S(1)} %copy-done.2, s32[512]{0:T(512)S(1)} %copy-done.1), custom_call_target="tpu_custom_call" | custom-call | tf_op jit(solution)/shard_map/pallas_call | solution.py:409
  103.7 0.7 copy.7
Async XLA Ops:
  0.0 1.0 copy-start
  1.0 57.6 %copy-start.1 = (s32[512]{0:T(512)S(1)}, s32[512]{0:T(512)}, u32[]{:S(2)}) copy-start(s32[512]{0:T(512)} %own_ref.1) | copy-start | bytes 6148
  1.0 57.7 %copy-start.2 = (s32[64]{0:T(128)S(1)}, s32[64]{0:T(128)}, u32[]{:S(2)}) copy-start(s32[64]{0:T(128)} %doc_ref.1) | copy-start | bytes 772

commit v2 on v1

--- a/solution.py
+++ b/solution.py
@@ -11,16 +11,16 @@
 NEG_FILL = -1e30
 DOC_MOST = 2048
 MESH = pl.DeviceIdType.MESH
-PIECES = 4
+PIECES = 8
 X_FIRST = (0, 1)
-Y_FIRST = (2, 3)
-GO_RIGHT = (0, 2)
-GO_LEFT = (1, 3)
+Y_FIRST = (2, 3, 4, 5, 6, 7)
+GO_RIGHT = (0, 2, 4, 6)
+GO_LEFT = (1, 3, 5, 7)
 HEAD_CHUNK = 2
 
 
-def gather_kernel(cfg, tok_hbm, qw_hbm, kw_hbm, qbuf, kv_out,
-                  tok, wq, wk, kvwin, load_sem, w_sem, tsend, trecv, ksend, krecv):
+def gather_kernel(cfg, tok_hbm, qw_hbm, kw_hbm, q_out, kv_out,
+                  tok, wq, wk, kvs, load_sem, w_sem, tsend, trecv, ksend, krecv):
     n_ctx, n_x, reach, rows, share, depth, heads, hd, blk, n_docs = cfg
     me = lax.axis_index("ctx")
     g = lax.axis_index("tp")
@@ -32,7 +32,6 @@
     xo = (x + 2) % n_x
     yo = 1 - y
     chunk_rows = 2 * share
-    per_dev = rows // blk
     part = depth // PIECES
 
     def shard_rows(yy, xx):
@@ -91,41 +90,47 @@
         send(right, y, x, p)
         send(left, y, x, p)
 
+    for d in range(1, reach + 1):
+        def clear(d=d):
+            kvs[d][...] = jnp.zeros(kvs[d].shape, jnp.bfloat16)
+        pl.when(me // 2 < d)(clear)
+
     ksent = []
     chunk_x = (x, xl, xr, xo)
 
     def chunk_at(k):
         return pl.ds(pl.multiple_of(chunk_x[k] * chunk_rows, chunk_rows), chunk_rows)
 
-    def kv_copy(target, src_slot, dst_slot, k, sem):
+    def kv_copy(target, src_d, dst_d, half, k, sem):
         return pltpu.make_async_remote_copy(
-            src_ref=kvwin.at[src_slot, chunk_at(k), :],
-            dst_ref=kvwin.at[dst_slot, chunk_at(k), :],
-            send_sem=ksend.at[sem], recv_sem=krecv.at[dst_slot * 4 + k],
+            src_ref=kvs[src_d].at[half, chunk_at(k), :],
+            dst_ref=kvs[dst_d].at[half, chunk_at(k), :],
+            send_sem=ksend.at[sem], recv_sem=krecv.at[dst_d * 8 + half * 4 + k],
             device_id={"ctx": target}, device_id_type=MESH)
 
-    def kv_send(target, src_slot, dst_slot, k):
-        c = kv_copy(target, src_slot, dst_slot, k, len(ksent))
-        c.start()
-        ksent.append(c)
-
-    def kv_got(slot, k):
-        kv_copy(me, slot, slot, k, 0).wait_recv()
+    def kv_send(target, src_d, dst_d, k, when):
+        c = kv_copy(target, src_d, dst_d, core, k, len(ksent))
+        pl.when(when)(c.start)
+        ksent.append((c, when))
+
+    def kv_got(d, half, k):
+        kv_copy(me, d, d, half, k, 0).wait_recv()
 
     up = (me + 2) % n_ctx
     twin = me + 1 - 2 * core
+    chip = me // 2
+    last = n_ctx // 2 - 1
 
     def kv_step(step):
         for d in range(0, reach + 1):
             k = step - d
             if k < 0 or k > 3:
                 continue
-            slot = d * 2 + core
             if d > 0:
-                kv_got(slot, k)
+                pl.when(chip >= d)(functools.partial(kv_got, d, core, k))
             if d < reach:
-                kv_send(up, slot, slot + 2, k)
-            kv_send(twin, slot, slot, k)
+                kv_send(up, d, d + 1, k, (chip >= d) & (chip < last))
+            kv_send(twin, d, d, k, chip >= d)
 
     def project(k):
         at = chunk_at(k)
@@ -134,7 +139,7 @@
             return acc + jnp.dot(tok[p, at, :], wk[p], preferred_element_type=jnp.float32)
 
         kv = lax.fori_loop(0, PIECES, kv_part, jnp.zeros((chunk_rows, 2 * hd), jnp.float32))
-        kvwin[core, at, :] = kv.astype(jnp.bfloat16)
+        kvs[0][core, at, :] = kv.astype(jnp.bfloat16)
         kv_step(k)
 
         def q_part(p, acc):
@@ -143,7 +148,7 @@
         q = lax.fori_loop(0, PIECES, q_part, jnp.zeros((chunk_rows, heads * hd), jnp.float32))
         q = q.astype(jnp.bfloat16)
         for h in range(heads):
-            qbuf[h, at, :] = q[:, h * hd:(h + 1) * hd]
+            q_out[h, at, :] = q[:, h * hd:(h + 1) * hd]
 
     for p in Y_FIRST:
         got(yo, x, p)
@@ -194,16 +199,20 @@
         got(yo, xo, p)
     project(3)
 
-    for m in range(1, reach + 1):
-        kv_step(3 + m)
+    def twin_got(d):
+        for k in range(4):
+            kv_got(d, 1 - core, k)
+
     for d in range(reach + 1):
-        for k in range(4):
-            kv_got(d * 2 + 1 - core, k)
-    kv_out[...] = kvwin[...]
+        if d > 0:
+            kv_step(3 + d)
+        pl.when(chip >= d)(functools.partial(twin_got, d))
+        for half in range(2):
+            kv_out[(2 * d + half) * rows:(2 * d + half + 1) * rows, :] = kvs[d][half]
     for c in sent:
         c.wait_send()
-    for c in ksent:
-        c.wait_send()
+    for c, when in ksent:
+        pl.when(when)(c.wait_send)
 
 
 def attend_kernel(cfg, qbuf, kvwin, doc_ref, own_ref, out_ref,
@@ -262,55 +271,52 @@
         (out_row // blk == rank) & (out_row % blk == slot_lane % blk), 1.0, 0.0
     ).astype(jnp.bfloat16)
 
-    mbuf[...] = jnp.full(mbuf.shape, NEG_FILL, jnp.float32)
-
-    def window_slot(t):
-        return ((t - core + 1) // 2) * 2 + (core + t) % 2
-
-    def score(t):
-        slot = window_slot(t)
-        key_place = ((me + n_ctx - t) % n_ctx) * rows + lane_place
-        allowed = (key_place >= row_start) & (key_place <= row_place)
-
-        def one(h, carry):
-            s = lax.dot_general(qbuf[h], kvwin[slot, :, 0:hd], (((1,), (1,)), ((), ())),
-                                preferred_element_type=jnp.float32)
-            s = jnp.where(allowed, s, NEG_FILL)
-            sbuf[h, t] = s
-            m = mbuf[h]
-            for c in range(rows // 128):
-                m = jnp.maximum(m, s[:, c * 128:(c + 1) * 128])
-            mbuf[h] = m
-            return carry
-
-        lax.fori_loop(0, heads, one, 0)
-
-    for t in range(2 * reach + 1):
-        score(t)
-
     scale = math.log2(math.e) / math.sqrt(hd)
     half = rows // 2
     asent = []
 
-    def finish(h, column):
-        for r in range(2):
-            at = pl.ds(r * half, half)
+    span = 2 * rows
+    places = jnp.concatenate([lane_place, lane_place + rows], axis=1)
+    mbuf[...] = jnp.full(mbuf.shape, NEG_FILL, jnp.float32)
+
+    def score(d, carry):
+        first = ((me - core + n_ctx - 2 * d) % n_ctx) * rows
+        key_place = places + first
+        allowed = (key_place >= row_start) & (key_place <= row_place)
+        keys = kvwin[pl.ds(pl.multiple_of(d * span, span), span), 0:hd]
+        for h in range(heads):
+            s = lax.dot_general(qbuf[h], keys, (((1,), (1,)), ((), ())),
+                                preferred_element_type=jnp.float32)
+            s = jnp.where(allowed, s, NEG_FILL)
+            sbuf[h, d] = s
+            m = mbuf[h]
+            for j in range(span // 128):
+                m = jnp.maximum(m, s[:, j * 128:(j + 1) * 128])
+            mbuf[h] = m
+        return carry
+
+    lax.fori_loop(0, reach + 1, score, 0)
+
+    def finish(chunk):
+        def one(index, carry):
+            c = index // 2
+            h = chunk * HEAD_CHUNK + c
+            at = pl.ds(pl.multiple_of((index % 2) * half, half), half)
             top = jnp.max(mbuf[h, at, :], axis=1, keepdims=True)
-
-            def step(t, carry):
-                total, acc = carry
-                w = jnp.exp2((sbuf[h, t, at, :] - top) * scale)
-                for c in range(rows // 128):
-                    total = total + w[:, c * 128:(c + 1) * 128]
-                acc = acc + jnp.dot(w.astype(jnp.bfloat16), kvwin[window_slot(t), :, hd:2 * hd],
+            total = jnp.zeros((half, 128), jnp.float32)
+            acc = jnp.zeros((half, hd), jnp.float32)
+            for d in range(reach + 1):
+                w = jnp.exp2((sbuf[h, d, at, :] - top) * scale)
+                for j in range(span // 128):
+                    total = total + w[:, j * 128:(j + 1) * 128]
+                acc = acc + jnp.dot(w.astype(jnp.bfloat16),
+                                    kvwin[d * span:(d + 1) * span, hd:2 * hd],
                                     preferred_element_type=jnp.float32)
-                return total, acc
-
-            total, acc = lax.fori_loop(0, 2 * reach + 1, step,
-                                       (jnp.zeros((half, 128), jnp.float32),
-                                        jnp.zeros((half, hd), jnp.float32)))
             value = acc / jnp.sum(total, axis=1, keepdims=True)
-            obuf[at, column * hd:(column + 1) * hd] = value.astype(jnp.bfloat16)
+            obuf[c, at, :] = value.astype(jnp.bfloat16)
+            return carry
+
+        lax.fori_loop(0, 2 * HEAD_CHUNK, one, 0)
 
     wide = HEAD_CHUNK * hd
 
@@ -334,10 +340,10 @@
     chunks = heads // HEAD_CHUNK
     my_slot = pl.ds(pl.multiple_of(me * blk, blk), blk)
     for chunk in range(chunks):
+        finish(chunk)
         for c in range(HEAD_CHUNK):
-            finish(chunk * HEAD_CHUNK + c, c)
-        sendbuf[chunk] = jnp.dot(pmat[...], obuf[...],
-                                 preferred_element_type=jnp.float32).astype(jnp.bfloat16)
+            sendbuf[chunk, :, c * hd:(c + 1) * hd] = jnp.dot(
+                pmat[...], obuf[c], preferred_element_type=jnp.float32).astype(jnp.bfloat16)
 
         def go(d, carry):
             a_copy(chunk, d).start()
@@ -381,20 +387,20 @@
     chunks = heads // HEAD_CHUNK
     wide = HEAD_CHUNK * hd
     bf, f32 = jnp.bfloat16, jnp.float32
-    n_tok = 12 + 4 * len(Y_FIRST) + 4 * len(X_FIRST) + 8
+    n_tok = 10 * PIECES
     n_kv = 4 * (2 * reach + 1)
     dma = pltpu.SemaphoreType.DMA
     q, kv = pl.pallas_call(
         functools.partial(gather_kernel, cfg),
         out_shape=(jax.ShapeDtypeStruct((heads, rows, hd), bf),
-                   jax.ShapeDtypeStruct((slots, rows, 2 * hd), bf)),
+                   jax.ShapeDtypeStruct((slots * rows, 2 * hd), bf)),
         in_specs=[pl.BlockSpec(memory_space=pl.ANY)] * 3,
         out_specs=[pl.BlockSpec(memory_space=pltpu.VMEM)] * 2,
         scratch_shapes=[
             pltpu.VMEM((PIECES, rows, part), bf),
             pltpu.VMEM((PIECES, part, heads * hd), bf),
             pltpu.VMEM((PIECES, part, 2 * hd), bf),
-            pltpu.VMEM((slots, rows, 2 * hd), bf),
+            [pltpu.VMEM((2, rows, 2 * hd), bf) for _ in range(reach + 1)],
             dma((PIECES,)),
             dma((2 * PIECES,)),
             dma((n_tok,)),
@@ -413,9 +419,9 @@
         + [pl.BlockSpec(memory_space=pltpu.SMEM)] * 2,
         out_specs=pl.BlockSpec(memory_space=pltpu.VMEM),
         scratch_shapes=[
-            pltpu.VMEM((heads, 2 * reach + 1, rows, rows), f32),
+            pltpu.VMEM((heads, reach + 1, rows, 2 * rows), f32),
             pltpu.VMEM((heads, rows, 128), f32),
-            pltpu.VMEM((rows, wide), bf),
+            pltpu.VMEM((HEAD_CHUNK, rows, hd), bf),
             pltpu.VMEM((chunks, n_ctx * blk, wide), bf),
             pltpu.VMEM((chunks, n_ctx * blk, wide), bf),
             pltpu.VMEM((n_ctx * blk, rows), bf),

time: 104 us -> 87.8 us (0.84)
  Pallas kernels: 103 us -> 85.9 us
    pallas_call x1, Pallas kernels: 57.6 us -> 48.9 us  [body(): pl.pallas_call(functools.partial(gather_kernel, cfg), out_shape=(jax.Shap...]
    pallas_call x1, Pallas kernels: 44.9 us -> 37 us  [body(): pl.pallas_call(functools.partial(attend_kernel, cfg), out_shape=jax.Shape...]
where the time goes in v2:
time: 87.8 us; the launch traced here: 87.7 us
  Pallas kernels  85.9 us (98%)
  local copies, waits for them, and re-layouts  1.75 us (2%)
    pallas_call x1, Pallas kernels, body(): pl.pallas_call(functools.partial(gather_kernel, cfg), out_shape=(jax.Shap...  48.9 us
    pallas_call x1, Pallas kernels, body(): pl.pallas_call(functools.partial(attend_kernel, cfg), out_shape=jax.Shape...  37 us

profile of v2, /device:TPU:1, one launch (start us, length us, event | category | flops | bytes accessed | tf_op | source)
XLA Modules:
  0.0 87.7 jit_solution(4471618496671027245)
XLA Ops:
  0.0 0.0 copy-start
  0.0 1.0 %copy-done = bf16[32,8192]{1,0:T(8,128)(2,1)S(1)} copy-done((bf16[32,8192]{1,0:T(8,128)(2,1)S(1)}, bf16[32,8192]{1,0:T(8,128)(2,1)}, u32[]{:S(2)}) %copy-start) | copy-done | bytes 524312
  1.0 0.0 copy-start.1
  1.0 0.0 copy-start.2
  1.0 48.9 %shard_map.55 = (bf16[4,256,128]{2,1,0:T(8,128)(2,1)S(1)}, bf16[2560,256]{1,0:T(8,128)(2,1)S(1)}) custom-call(bf16[32,8192]{1,0:T(8,128)(2,1)S(1)} %copy-done, bf16[8192,512]{1,0:T(8,128)(2,1)} %qw_hbm.1, bf16[8192,256]{1,0:T(8,128)(2,1)} %kw_hbm.1), custom_call_target="tpu_custom_call" | custom-call | tf_op jit(solution)/shard_map/pallas_call | solution.py:393
  49.9 0.0 copy-done.1
  49.9 0.0 copy-done.2
  49.9 37.0 %shard_map.56 = bf16[256,512]{1,0:T(8,128)(2,1)S(1)} custom-call(bf16[4,256,128]{2,1,0:T(8,128)(2,1)S(1)} %get-tuple-element.7.qbuf, bf16[2560,256]{1,0:T(8,128)(2,1)S(1)} %get-tuple-element.8.kvwin, s32[64]{0:T(128)S(1)} %copy-done.2, s32[512]{0:T(512)S(1)} %copy-done.1), custom_call_target="tpu_custom_call" | custom-call | tf_op jit(solution)/shard_map/pallas_call | solution.py:415
  87.0 0.7 copy.7
Async XLA Ops:
  0.0 1.0 %copy-start = (bf16[32,8192]{1,0:T(8,128)(2,1)S(1)}, bf16[32,8192]{1,0:T(8,128)(2,1)}, u32[]{:S(2)}) copy-start(bf16[32,8192]{1,0:T(8,128)(2,1)} %tok_hbm.1) | copy-start | bytes 1572868
  1.0 48.9 %copy-start.1 = (s32[512]{0:T(512)S(1)}, s32[512]{0:T(512)}, u32[]{:S(2)}) copy-start(s32[512]{0:T(512)} %own_ref.1) | copy-start | bytes 6148
  1.0 48.9 %copy-start.2 = (s32[64]{0:T(128)S(1)}, s32[64]{0:T(128)}, u32[]{:S(2)}) copy-start(s32[64]{0:T(128)} %doc_ref.1) | copy-start | bytes 772

commit v3 on v2

--- a/solution.py
+++ b/solution.py
@@ -11,11 +11,11 @@
 NEG_FILL = -1e30
 DOC_MOST = 2048
 MESH = pl.DeviceIdType.MESH
-PIECES = 8
-X_FIRST = (0, 1)
-Y_FIRST = (2, 3, 4, 5, 6, 7)
-GO_RIGHT = (0, 2, 4, 6)
-GO_LEFT = (1, 3, 5, 7)
+PIECES = 4
+X_FIRST = (0,)
+Y_FIRST = (1, 2, 3)
+GO_RIGHT = (0, 2)
+GO_LEFT = (1, 3)
 HEAD_CHUNK = 2
 
 
@@ -279,12 +279,12 @@
     places = jnp.concatenate([lane_place, lane_place + rows], axis=1)
     mbuf[...] = jnp.full(mbuf.shape, NEG_FILL, jnp.float32)
 
-    def score(d, carry):
+    def score(chunk, d, carry):
         first = ((me - core + n_ctx - 2 * d) % n_ctx) * rows
         key_place = places + first
         allowed = (key_place >= row_start) & (key_place <= row_place)
         keys = kvwin[pl.ds(pl.multiple_of(d * span, span), span), 0:hd]
-        for h in range(heads):
+        for h in range(chunk * HEAD_CHUNK, (chunk + 1) * HEAD_CHUNK):
             s = lax.dot_general(qbuf[h], keys, (((1,), (1,)), ((), ())),
                                 preferred_element_type=jnp.float32)
             s = jnp.where(allowed, s, NEG_FILL)
@@ -294,8 +294,6 @@
                 m = jnp.maximum(m, s[:, j * 128:(j + 1) * 128])
             mbuf[h] = m
         return carry
-
-    lax.fori_loop(0, reach + 1, score, 0)
 
     def finish(chunk):
         def one(index, carry):
@@ -336,14 +334,17 @@
             send_sem=asend.at[chunk * n_ctx + d], recv_sem=arecv.at[chunk * n_ctx + d],
             device_id={"ctx": source}, device_id_type=MESH).wait_recv()
 
-    pl.semaphore_wait(barrier, n_ctx - 1)
     chunks = heads // HEAD_CHUNK
     my_slot = pl.ds(pl.multiple_of(me * blk, blk), blk)
     for chunk in range(chunks):
+        lax.fori_loop(0, reach + 1, functools.partial(score, chunk), 0)
         finish(chunk)
         for c in range(HEAD_CHUNK):
             sendbuf[chunk, :, c * hd:(c + 1) * hd] = jnp.dot(
                 pmat[...], obuf[c], preferred_element_type=jnp.float32).astype(jnp.bfloat16)
+
+        if chunk == 0:
+            pl.semaphore_wait(barrier, n_ctx - 1)
 
         def go(d, carry):
             a_copy(chunk, d).start()

time: 87.8 us -> 85 us (0.968)
  Pallas kernels: 85.9 us -> 83.1 us
    pallas_call x1, Pallas kernels: 48.9 us -> 47 us  [body(): pl.pallas_call(functools.partial(gather_kernel, cfg), out_shape=(jax.Shap...]
    pallas_call x1, Pallas kernels: 37 us -> 36.1 us  [body(): pl.pallas_call(functools.partial(attend_kernel, cfg), out_shape=jax.Shape...]
where the time goes in v3:
time: 85 us; the launch traced here: 84.8 us
  Pallas kernels  83.1 us (98%)
  local copies, waits for them, and re-layouts  1.75 us (2%)
    pallas_call x1, Pallas kernels, body(): pl.pallas_call(functools.partial(gather_kernel, cfg), out_shape=(jax.Shap...  47 us
    pallas_call x1, Pallas kernels, body(): pl.pallas_call(functools.partial(attend_kernel, cfg), out_shape=jax.Shape...  36.1 us
    unnamed x7, local copies, waits for them, and re-layouts  1.75 us

profile of v3, /device:TPU:1, one launch (start us, length us, event | category | flops | bytes accessed | tf_op | source)
XLA Modules:
  0.0 84.8 jit_solution(10087449107650154139)
XLA Ops:
  0.0 0.0 copy-start
  0.0 1.0 %copy-done = bf16[32,8192]{1,0:T(8,128)(2,1)S(1)} copy-done((bf16[32,8192]{1,0:T(8,128)(2,1)S(1)}, bf16[32,8192]{1,0:T(8,128)(2,1)}, u32[]{:S(2)}) %copy-start) | copy-done | bytes 524312
  1.0 0.0 copy-start.1
  1.0 0.0 copy-start.2
  1.0 47.0 %shard_map.55 = (bf16[4,256,128]{2,1,0:T(8,128)(2,1)S(1)}, bf16[2560,256]{1,0:T(8,128)(2,1)S(1)}) custom-call(bf16[32,8192]{1,0:T(8,128)(2,1)S(1)} %copy-done, bf16[8192,512]{1,0:T(8,128)(2,1)} %qw_hbm.1, bf16[8192,256]{1,0:T(8,128)(2,1)} %kw_hbm.1), custom_call_target="tpu_custom_call" | custom-call | tf_op jit(solution)/shard_map/pallas_call | solution.py:394
  48.0 0.0 copy-done.1
  48.0 0.0 copy-done.2
  48.0 36.1 %shard_map.56 = bf16[256,512]{1,0:T(8,128)(2,1)S(1)} custom-call(bf16[4,256,128]{2,1,0:T(8,128)(2,1)S(1)} %get-tuple-element.7.qbuf, bf16[2560,256]{1,0:T(8,128)(2,1)S(1)} %get-tuple-element.8.kvwin, s32[64]{0:T(128)S(1)} %copy-done.2, s32[512]{0:T(512)S(1)} %copy-done.1), custom_call_target="tpu_custom_call" | custom-call | tf_op jit(solution)/shard_map/pallas_call | solution.py:416
  84.1 0.7 copy.7
Async XLA Ops:
  0.0 1.0 %copy-start = (bf16[32,8192]{1,0:T(8,128)(2,1)S(1)}, bf16[32,8192]{1,0:T(8,128)(2,1)}, u32[]{:S(2)}) copy-start(bf16[32,8192]{1,0:T(8,128)(2,1)} %tok_hbm.1) | copy-start | bytes 1572868
  1.0 47.0 %copy-start.1 = (s32[512]{0:T(512)S(1)}, s32[512]{0:T(512)}, u32[]{:S(2)}) copy-start(s32[512]{0:T(512)} %own_ref.1) | copy-start | bytes 6148
  1.0 47.0 %copy-start.2 = (s32[64]{0:T(128)S(1)}, s32[64]{0:T(128)}, u32[]{:S(2)}) copy-start(s32[64]{0:T(128)} %doc_ref.1) | copy-start | bytes 772

commit v4 on v3

--- a/solution.py
+++ b/solution.py
@@ -12,8 +12,8 @@
 DOC_MOST = 2048
 MESH = pl.DeviceIdType.MESH
 PIECES = 4
-X_FIRST = (0,)
-Y_FIRST = (1, 2, 3)
+X_FIRST = (0, 1)
+Y_FIRST = (2, 3)
 GO_RIGHT = (0, 2)
 GO_LEFT = (1, 3)
 HEAD_CHUNK = 2

time: 85 us -> 91.6 us (1.078)
  Pallas kernels: 83.1 us -> 89.7 us
    pallas_call x1, Pallas kernels: 47 us -> 53.9 us  [body(): pl.pallas_call(functools.partial(gather_kernel, cfg), out_shape=(jax.Shap...]
where the time goes in v4:
time: 91.6 us; the launch traced here: 91.4 us
  Pallas kernels  89.7 us (98%)
  local copies, waits for them, and re-layouts  1.75 us (2%)
    pallas_call x1, Pallas kernels, body(): pl.pallas_call(functools.partial(gather_kernel, cfg), out_shape=(jax.Shap...  53.9 us
    pallas_call x1, Pallas kernels, body(): pl.pallas_call(functools.partial(attend_kernel, cfg), out_shape=jax.Shape...  35.7 us

profile of v4, /device:TPU:1, one launch (start us, length us, event | category | flops | bytes accessed | tf_op | source)
XLA Modules:
  0.0 91.4 jit_solution(5831185178966107024)
XLA Ops:
  0.0 0.0 copy-start
  0.0 1.0 %copy-done = bf16[32,8192]{1,0:T(8,128)(2,1)S(1)} copy-done((bf16[32,8192]{1,0:T(8,128)(2,1)S(1)}, bf16[32,8192]{1,0:T(8,128)(2,1)}, u32[]{:S(2)}) %copy-start) | copy-done | bytes 524312
  1.0 0.0 copy-start.1
  1.0 0.0 copy-start.2
  1.0 53.9 %shard_map.55 = (bf16[4,256,128]{2,1,0:T(8,128)(2,1)S(1)}, bf16[2560,256]{1,0:T(8,128)(2,1)S(1)}) custom-call(bf16[32,8192]{1,0:T(8,128)(2,1)S(1)} %copy-done, bf16[8192,512]{1,0:T(8,128)(2,1)} %qw_hbm.1, bf16[8192,256]{1,0:T(8,128)(2,1)} %kw_hbm.1), custom_call_target="tpu_custom_call" | custom-call | tf_op jit(solution)/shard_map/pallas_call | solution.py:394
  55.0 0.0 copy-done.1
  55.0 0.0 copy-done.2
  55.0 35.7 %shard_map.56 = bf16[256,512]{1,0:T(8,128)(2,1)S(1)} custom-call(bf16[4,256,128]{2,1,0:T(8,128)(2,1)S(1)} %get-tuple-element.7.qbuf, bf16[2560,256]{1,0:T(8,128)(2,1)S(1)} %get-tuple-element.8.kvwin, s32[64]{0:T(128)S(1)} %copy-done.2, s32[512]{0:T(512)S(1)} %copy-done.1), custom_call_target="tpu_custom_call" | custom-call | tf_op jit(solution)/shard_map/pallas_call | solution.py:416
  90.7 0.7 copy.7
Async XLA Ops:
  0.0 1.0 %copy-start = (bf16[32,8192]{1,0:T(8,128)(2,1)S(1)}, bf16[32,8192]{1,0:T(8,128)(2,1)}, u32[]{:S(2)}) copy-start(bf16[32,8192]{1,0:T(8,128)(2,1)} %tok_hbm.1) | copy-start | bytes 1572868
  1.0 53.9 %copy-start.1 = (s32[512]{0:T(512)S(1)}, s32[512]{0:T(512)}, u32[]{:S(2)}) copy-start(s32[512]{0:T(512)} %own_ref.1) | copy-start | bytes 6148
  1.0 53.9 %copy-start.2 = (s32[64]{0:T(128)S(1)}, s32[64]{0:T(128)}, u32[]{:S(2)}) copy-start(s32[64]{0:T(128)} %doc_ref.1) | copy-start | bytes 772
